TPU v7x, 512 devices: a whole 4x4x16 slice. The times are simulated.
512 devices in a mesh: space: 32 (over x, y, core), member: 16 (over z).
Axes of the slice: x: 4, y: 4, z: 16, core: 2. Of those that a mesh axis runs over, the one named last changes fastest.
Arguments:
- obs_pert: bfloat16 [80, 65536], P('member', 'space'), may hold values from -6 to 6
- innovation: bfloat16 [65536], P('space'), may hold values from -6 to 6
- obs_prec: bfloat16 [65536], P('space'), may hold values from 1 to 100
- obs_lists: int32 [6144, 256], P('space'), may hold values from 0 to 6143
- loc_weight: bfloat16 [6144, 256], P('space'), may hold values from 0.049804688 to 1
- send_rows: int32 [32, 16, 32], P('space'), may hold values from 0 to 11
- ocean_src: int32 [3072, 2], P('space'), may hold values from 0 to 511, as said below
- ocean_frac: float32 [3072], P('space'), may hold values from 0 to 1
- ocean_ens: bfloat16 [80, 3072, 2048], P(None, 'space', 'member'), may hold values from -6 to 6
Outputs:
- ocean_anal: bfloat16 [80, 3072, 2048], P(None, 'space', 'member')
Inputs may be any that keep to these rules, and one draw needn't show every extreme that they name: `ocean_src`: the two slots of one ocean block differ.
All inputs are finite; a program needn't handle non-finite values.
Results may differ from a plain program's by a relative error of at most 0.0064.
Values may be sent and summed in bfloat16 or wider, within the bound.
No kernel may reach another device: no remote copies, remote signals or barrier semaphores. Data moves between devices by JAX's collectives and lax.ppermute only.
A program may use at most 64 MiB of HBM per device.

v0:
```python
import jax
import jax.numpy as jnp
from jax import lax
from jax.sharding import PartitionSpec as P

ITERS = 12


def padded(cells, sides, width):
    for axis, dim in sides:
        count = lax.axis_size(axis)
        head = lax.slice_in_dim(cells, 0, width, axis=dim)
        tail = lax.slice_in_dim(cells, cells.shape[dim] - width, cells.shape[dim], axis=dim)
        cells = jnp.concatenate(
            [
                lax.ppermute(tail, axis, [(i, (i + 1) % count) for i in range(count)]),
                cells,
                lax.ppermute(head, axis, [((i + 1) % count, i) for i in range(count)]),
            ],
            axis=dim,
        )
    return cells


def copy_for_each(array, axis):
    devices = lax.axis_size(axis)
    return lax.all_to_all(
        jnp.broadcast_to(array[None], (devices, *array.shape)), axis, 0, 0, tiled=True
    )


def joined_along(pieces, dim):
    pieces = jnp.moveaxis(pieces, 0, dim)
    dims = pieces.shape
    return pieces.reshape(*dims[:dim], dims[dim] * dims[dim + 1], *dims[dim + 2 :])


def gather_directly(array, axis, dim):
    pieces = copy_for_each(array, axis)
    return joined_along(pieces, dim)


def transform(local_obs, loc_sel, innov_sel, prec_sel):
    members = local_obs.shape[0]
    obs_f32 = local_obs.astype(jnp.float32)
    obs_weight = loc_sel.astype(jnp.float32) * prec_sel.astype(jnp.float32)
    weighted = obs_f32 * obs_weight[None]
    gram = jnp.einsum("ibl,jbl->bij", weighted, obs_f32, precision=lax.Precision.HIGHEST)
    pulled = jnp.einsum(
        "ibl,bl->bi", weighted, innov_sel.astype(jnp.float32), precision=lax.Precision.HIGHEST
    )
    identity = jnp.eye(members, dtype=jnp.float32)
    precision_mat = (members - 1.0) * identity + gram
    scale_sum = jnp.trace(precision_mat, axis1=1, axis2=2)
    root_start = precision_mat / scale_sum[:, None, None]
    inverse_start = jnp.broadcast_to(identity, precision_mat.shape)

    def newton(iteration, carry):
        root_iter, inverse_iter = carry
        correction = 1.5 * identity - 0.5 * jnp.einsum(
            "bij,bjk->bik", inverse_iter, root_iter, precision=lax.Precision.HIGHEST
        )
        root_next = jnp.einsum(
            "bij,bjk->bik", root_iter, correction, precision=lax.Precision.HIGHEST
        )
        inverse_next = jnp.einsum(
            "bij,bjk->bik", correction, inverse_iter, precision=lax.Precision.HIGHEST
        )
        return (root_next, inverse_next)

    root_iter, inverse_iter = lax.fori_loop(0, ITERS, newton, (root_start, inverse_start))
    spread = jnp.sqrt((members - 1.0) / scale_sum)[:, None, None] * inverse_iter
    half_way = jnp.einsum("bij,bj->bi", inverse_iter, pulled, precision=lax.Precision.HIGHEST)
    mean_weight = (
        jnp.einsum("bij,bj->bi", inverse_iter, half_way, precision=lax.Precision.HIGHEST)
        / scale_sum[:, None]
    )
    return (spread + mean_weight[:, :, None]).astype(jnp.bfloat16)


def apply_weights(ensemble, mixed):
    ens_mean = jnp.mean(ensemble, axis=0, dtype=jnp.float32)
    deviation = (ensemble.astype(jnp.float32) - ens_mean[None]).astype(jnp.bfloat16)
    product = jnp.einsum("jol,oji->iol", deviation, mixed, preferred_element_type=jnp.float32)
    return (ens_mean[None] + product).astype(jnp.bfloat16)


def shards(
    obs_pert,
    innovation,
    obs_prec,
    obs_lists,
    loc_weight,
    send_rows,
    ocean_src,
    ocean_frac,
    ocean_ens,
):
    n_member = lax.axis_size("member")
    n_space = lax.axis_size("space")
    member_idx = lax.axis_index("member")
    tile_obs = obs_pert.shape[1]
    stacked = jnp.stack([innovation, obs_prec])
    pert_rim, info_rim = (
        padded(obs_pert, (("space", 1),), tile_obs),
        padded(stacked, (("space", 1),), tile_obs),
    )
    blocks = obs_lists.shape[0]
    group_len = blocks // n_member
    lists_mine = lax.dynamic_slice_in_dim(obs_lists, member_idx * group_len, group_len, 0)
    loc_mine = lax.dynamic_slice_in_dim(loc_weight, member_idx * group_len, group_len, 0)
    all_members = gather_directly(pert_rim, "member", 0)
    local_obs = all_members[:, lists_mine]
    innov_sel = info_rim[0][lists_mine]
    prec_sel = info_rim[1][lists_mine]
    weights = transform(local_obs, loc_mine, innov_sel, prec_sel)
    row_choice = lax.dynamic_index_in_dim(send_rows[0], member_idx, 0, keepdims=False)
    picked = weights[row_choice]
    arrived = lax.all_to_all(picked, "space", split_axis=0, concat_axis=0, tiled=True)
    mine_one = ocean_src[:, 0] // n_space == member_idx
    mine_two = ocean_src[:, 1] // n_space == member_idx
    coef_one = jnp.where(mine_one, 1.0 - ocean_frac, 0.0)[:, None, None]
    coef_two = jnp.where(mine_two, ocean_frac, 0.0)[:, None, None]
    take_one = arrived[ocean_src[:, 0] % n_space].astype(jnp.float32)
    take_two = arrived[ocean_src[:, 1] % n_space].astype(jnp.float32)
    partial_mix = coef_one * take_one + coef_two * take_two
    mixed = lax.psum(partial_mix, "member").astype(jnp.bfloat16)
    return apply_weights(ocean_ens, mixed)


def solution(mesh):
    return jax.shard_map(
        shards,
        mesh=mesh,
        in_specs=(
            P("member", "space"),
            P("space"),
            P("space"),
            P("space", None),
            P("space", None),
            P("space", None, None),
            P("space", None),
            P("space"),
            P(None, "space", "member"),
        ),
        out_specs=P(None, "space", "member"),
        check_vma=False,
    )
```

profile of v0, /device:TPU:6, one launch (start us, length us, event | category | flops | bytes accessed | tf_op | source)
XLA Modules:
  0.0 276.2 jit_solution(2189907386546934300)
XLA Ops:
  0.0 1.9 collective-permute-start
  1.9 5.8 %collective-permute-start.1 = (bf16[5,2048]{1,0:T(8,128)(2,1)}, bf16[5,2048]{1,0:T(8,128)(2,1)S(1)}, u32[]{:S(2)}, u32[]{:S(2)}) collective-permute-start(bf16[5,2048]{1,0:T(8,128)(2,1)} %param.11), channel_id=1, source_target_pairs={{16,0},{32,16},{48,32},{64,48},{80,64},{96,80},{112,96},{128,112},... | collective-permute-start | bytes 61448 | tf_op jit(solution)/shard_map/ppermute | solution.py:18
  7.7 1.9 collective-permute-done.1
  10.3 1.3 broadcast_in_dim.23
  11.7 15.4 %all-to-all-start = ((bf16[16,5,6144]{2,1,0:T(8,128)(2,1)}), bf16[16,5,6144]{2,1,0:T(8,128)(2,1)}, u32[]{:S(2)}, u32[]{:S(2)}) async-start(bf16[16,5,6144]{2,1,0:T(8,128)(2,1)} %broadcast_in_dim.23), calls=%async_computation | async-start | bytes 3145728 | tf_op jit(solution)/shard_map/all_to_all | solution.py:27
  27.1 1.9 collective-permute-start.2
  29.1 5.8 %collective-permute-start.3 = (bf16[2,2048]{1,0:T(2,128)(2,1)S(1)}, bf16[2,2048]{1,0:T(2,128)(2,1)S(1)}, u32[]{:S(2)}, u32[]{:S(2)}) collective-permute-start(bf16[2,2048]{1,0:T(2,128)(2,1)S(1)} %pad_maximum_fusion.2), channel_id=1, source_target_pairs={{16,0},{32,16},{48,32},{64,48},{80,64},{96,80},{112,96},{128,112},... | collective-permute-start | bytes 24584 | tf_op jit(solution)/shard_map/ppermute | solution.py:18
  40.4 19.4 %gather_fusion.1 = bf16[3072]{0:T(1024)(128)(2,1)S(1)} fusion(bf16[6144]{0:T(1024)(128)(2,1)S(1)} %get-tuple-element.46, s32[3072]{0:T(1024)S(1)} %broadcast_clamp_fusion), kind=kCustom, calls=%fused_computation.1 | custom fusion | bytes 24576 | tf_op jit(solution)/shard_map/gather | solution.py:115
  59.7 19.4 %gather_fusion.2 = bf16[3072]{0:T(1024)(128)(2,1)S(1)} fusion(bf16[6144]{0:T(1024)(128)(2,1)S(1)} %get-tuple-element.45, s32[3072]{0:T(1024)S(1)} %broadcast_clamp_fusion), kind=kCustom, calls=%fused_computation.2 | custom fusion | bytes 24576 | tf_op jit(solution)/shard_map/gather | solution.py:114
  79.7 1.3 convert_multiply_fusion.3
  81.0 19.9 %all-to-all-done = bf16[16,5,6144]{2,1,0:T(8,128)(2,1)} async-done(((bf16[16,5,6144]{2,1,0:T(8,128)(2,1)}), bf16[16,5,6144]{2,1,0:T(8,128)(2,1)}, u32[]{:S(2)}, u32[]{:S(2)}) %all-to-all-start) | async-done | bytes 983072 | tf_op jit(solution)/shard_map/all_to_all | solution.py:27
  100.9 2.4 reshape.58
  103.3 1.8 copy.31
  105.1 11.5 %gather_fusion = bf16[3072,80]{1,0:T(8,128)(2,1)} fusion(bf16[80,6144]{0,1:T(8,128)(2,1)S(1)} %copy.31, s32[3072]{0:T(1024)S(1)} %broadcast_clamp_fusion), kind=kCustom, calls=%fused_computation | custom fusion | bytes 995328 | tf_op jit(solution)/shard_map/gather | solution.py:113
  116.6 1.4 copy.32
  118.1 1.5 select_reduce_fusion
  120.0 32.0 %while.13 = (s32[]{:T(128)}, f32[12,80,80]{1,2,0:T(8,128)S(1)}, f32[12,80,80]{2,1,0:T(8,128)S(1)}, s32[]{:T(128)}) while((s32[]{:T(128)}, f32[12,80,80]{1,2,0:T(8,128)S(1)}, f32[12,80,80]{2,1,0:T(8,128)S(1)}, s32[]{:T(128)}) %tuple.29), condition=%wide.region_3.4_spmd.clone, body=%wide.region_2.3_spmd.clone.sunk | while | flops 221350400 | bytes 4044853 | solution.py:71
  124.3 1.0 convolution_bitcast_fusion.2
  127.0 1.0 convolution_bitcast_fusion.2
  132.3 1.0 convolution_bitcast_fusion.2
  140.3 1.0 convolution_bitcast_fusion.2
  154.7 1.5 gather_fusion.3
  156.2 6.2 %all-to-all-start.1 = ((bf16[32,80,80]{2,1,0:T(8,128)(2,1)}), bf16[32,80,80]{2,1,0:T(8,128)(2,1)S(1)}, u32[]{:S(2)}, u32[]{:S(2)}) async-start(bf16[32,80,80]{2,1,0:T(8,128)(2,1)} %gather_fusion.3), calls=%async_computation.1 | async-start | bytes 1310720 | tf_op jit(solution)/shard_map/all_to_all | solution.py:119
  162.5 1.7 fusion.4
  164.1 8.9 %all-to-all-done.1 = bf16[32,80,80]{2,1,0:T(8,128)(2,1)S(1)} async-done(((bf16[32,80,80]{2,1,0:T(8,128)(2,1)}), bf16[32,80,80]{2,1,0:T(8,128)(2,1)S(1)}, u32[]{:S(2)}, u32[]{:S(2)}) %all-to-all-start.1) | async-done | bytes 409632 | tf_op jit(solution)/shard_map/all_to_all | solution.py:119
  173.9 3.5 %copy.34 = bf16[96,80,80]{0,2,1:T(8,128)(2,1)} copy(bf16[96,80,80]{2,1,0:T(8,128)(2,1)S(1)} %gather_fusion.4) | data formatting | bytes 2457600 | tf_op jit(solution)/shard_map/gather | solution.py:124
  178.3 3.5 %copy.35 = bf16[96,80,80]{0,2,1:T(8,128)(2,1)} copy(bf16[96,80,80]{2,1,0:T(8,128)(2,1)S(1)} %gather_fusion.5) | data formatting | bytes 2457600 | tf_op jit(solution)/shard_map/gather | solution.py:125
  181.8 2.5 multiply_add_fusion
  184.2 81.5 %all-reduce.1 = bf16[96,80,80]{0,2,1:T(8,128)(2,1)} all-reduce(f32[96,80,80]{0,2,1:T(8,128)S(1)} %multiply_add_fusion), channel_id=1, replica_groups=mesh['space'=32,'member'=16] {'member'}, use_global_device_ids=true, to_apply=%region_4.5 | all-reduce | flops 614400 | bytes 3686400 | tf_op jit(solution)/shard_map/psum | solution.py:127
  265.8 5.9 %copy.36 = bf16[96,80,80]{1,2,0:T(8,128)(2,1)S(1)} copy(bf16[96,80,80]{0,2,1:T(8,128)(2,1)} %all-reduce.1) | data formatting | bytes 2457600 | tf_op jit(solution)/shard_map/convert_element_type | solution.py:127
  271.7 2.8 fusion.6
  274.4 1.8 copy.38
  (133 shorter events, 39.2 us)
Async XLA Ops:
  0.0 7.7 %collective-permute-start = (bf16[5,2048]{1,0:T(8,128)(2,1)}, bf16[5,2048]{1,0:T(8,128)(2,1)S(1)}, u32[]{:S(2)}, u32[]{:S(2)}) collective-permute-start(bf16[5,2048]{1,0:T(8,128)(2,1)} %param.11), channel_id=1, source_target_pairs={{0,16},{16,32},{32,48},{48,64},{64,80},{80,96},{96,112},{112,128},... | collective-permute-start | bytes 61448 | tf_op jit(solution)/shard_map/ppermute | solution.py:16
  1.9 7.7 %collective-permute-start.1 = (bf16[5,2048]{1,0:T(8,128)(2,1)}, bf16[5,2048]{1,0:T(8,128)(2,1)S(1)}, u32[]{:S(2)}, u32[]{:S(2)}) collective-permute-start(bf16[5,2048]{1,0:T(8,128)(2,1)} %param.11), channel_id=1, source_target_pairs={{16,0},{32,16},{48,32},{64,48},{80,64},{96,80},{112,96},{128,112},... | collective-permute-start | bytes 61448 | tf_op jit(solution)/shard_map/ppermute | solution.py:18
  11.6 15.4 %copy-start.6 = (bf16[2048]{0:T(1024)(128)(2,1)S(1)}, bf16[2048]{0:T(1024)(128)(2,1)}, u32[]{:S(2)}) copy-start(bf16[2048]{0:T(1024)(128)(2,1)} %param.13) | copy-start | bytes 12292
  11.6 15.4 %copy-start.7 = (bf16[2048]{0:T(1024)(128)(2,1)S(1)}, bf16[2048]{0:T(1024)(128)(2,1)}, u32[]{:S(2)}) copy-start(bf16[2048]{0:T(1024)(128)(2,1)} %param.12) | copy-start | bytes 12292
  11.6 26.5 %copy-start = (bf16[80,96,128]{2,1,0:T(8,128)(2,1)S(1)}, bf16[80,96,128]{2,1,0:T(8,128)(2,1)}, u32[]{:S(2)}) copy-start(bf16[80,96,128]{2,1,0:T(8,128)(2,1)} %param.19) | copy-start | bytes 5898244
  11.6 26.8 %copy-start.8 = (s32[96,2]{0,1:T(2,128)S(1)}, s32[96,2]{0,1:T(2,128)}, u32[]{:S(2)}) copy-start(s32[96,2]{0,1:T(2,128)} %param.17) | copy-start | bytes 2308
  11.7 27.4 %copy-start.13 = (f32[96]{0:T(128)S(1)}, f32[96]{0:T(128)}, u32[]{:S(2)}) copy-start(f32[96]{0:T(128)} %param.18) | copy-start | bytes 1156
  11.7 89.2 %all-to-all-start = ((bf16[16,5,6144]{2,1,0:T(8,128)(2,1)}), bf16[16,5,6144]{2,1,0:T(8,128)(2,1)}, u32[]{:S(2)}, u32[]{:S(2)}) async-start(bf16[16,5,6144]{2,1,0:T(8,128)(2,1)} %broadcast_in_dim.23), calls=%async_computation | async-start | bytes 3145728 | tf_op jit(solution)/shard_map/all_to_all | solution.py:27
  27.1 13.0 %collective-permute-start.2 = (bf16[2,2048]{1,0:T(2,128)(2,1)S(1)}, bf16[2,2048]{1,0:T(2,128)(2,1)S(1)}, u32[]{:S(2)}, u32[]{:S(2)}) collective-permute-start(bf16[2,2048]{1,0:T(2,128)(2,1)S(1)} %pad_maximum_fusion.2), channel_id=1, source_target_pairs={{0,16},{16,32},{32,48},{48,64},{64,80},{80,96},{96,112},{112,128},... | collective-permute-start | bytes 24584 | tf_op jit(solution)/shard_map/ppermute | solution.py:16
  29.1 11.1 %collective-permute-start.3 = (bf16[2,2048]{1,0:T(2,128)(2,1)S(1)}, bf16[2,2048]{1,0:T(2,128)(2,1)S(1)}, u32[]{:S(2)}, u32[]{:S(2)}) collective-permute-start(bf16[2,2048]{1,0:T(2,128)(2,1)S(1)} %pad_maximum_fusion.2), channel_id=1, source_target_pairs={{16,0},{32,16},{48,32},{64,48},{80,64},{96,80},{112,96},{128,112},... | collective-permute-start | bytes 24584 | tf_op jit(solution)/shard_map/ppermute | solution.py:18
  118.0 1.9 copy-start.3
  120.0 32.0 %copy-start.4 = (f32[12,256]{1,0:T(8,128)S(1)}, f32[12,256]{1,0:T(8,128)}, u32[]{:S(2)}) copy-start(f32[12,256]{1,0:T(8,128)} %convert_multiply_fusion.3) | copy-start | bytes 36868
  120.0 32.0 %copy-start.5 = (bf16[12,256,1]{1,2,0:T(2,128)(2,1)S(1)}, bf16[12,256,1]{1,2,0:T(2,128)(2,1)}, u32[]{:S(2)}) copy-start(bf16[12,256,1]{1,2,0:T(2,128)(2,1)} %reshape.121) | copy-start | bytes 18436
  153.5 8.9 %copy-start.11 = (s32[96]{0:T(128)S(1)}, s32[96]{0:T(128)}, u32[]{:S(2)}) copy-start(s32[96]{0:T(128)} %get-tuple-element.55) | copy-start | bytes 1156
  153.5 8.9 %copy-start.12 = (s32[96]{0:T(128)S(1)}, s32[96]{0:T(128)}, u32[]{:S(2)}) copy-start(s32[96]{0:T(128)} %get-tuple-element.56) | copy-start | bytes 1156
  153.5 9.0 %copy-start.1 = (f32[96,128]{1,0:T(8,128)S(1)}, f32[96,128]{1,0:T(8,128)}, u32[]{:S(2)}) copy-start(f32[96,128]{1,0:T(8,128)} %broadcast_multiply_fusion) | copy-start | bytes 147460
  156.2 16.8 %all-to-all-start.1 = ((bf16[32,80,80]{2,1,0:T(8,128)(2,1)}), bf16[32,80,80]{2,1,0:T(8,128)(2,1)S(1)}, u32[]{:S(2)}, u32[]{:S(2)}) async-start(bf16[32,80,80]{2,1,0:T(8,128)(2,1)} %gather_fusion.3), calls=%async_computation.1 | async-start | bytes 1310720 | tf_op jit(solution)/shard_map/all_to_all | solution.py:119
  178.3 3.5 %copy-start.9 = (f32[96]{0:T(128)S(1)}, f32[96]{0:T(128)}, u32[]{:S(2)}) copy-start(f32[96]{0:T(128)} %get-tuple-element.53) | copy-start | bytes 1156
  178.3 3.5 %copy-start.10 = (f32[96]{0:T(128)S(1)}, f32[96]{0:T(128)}, u32[]{:S(2)}) copy-start(f32[96]{0:T(128)} %get-tuple-element.54) | copy-start | bytes 1156
  265.8 5.9 %copy-start.2 = (f32[96,128]{1,0:T(8,128)S(1)}, f32[96,128]{1,0:T(8,128)}, u32[]{:S(2)}) copy-start(f32[96,128]{1,0:T(8,128)} %broadcast_multiply_fusion) | copy-start | bytes 147460
where the time goes:
time: 277 us; the launch traced here: 276 us
  blocking collectives  81.5 us (29%)
  local copies, waits for them, and re-layouts  76.9 us (28%)
  matrix products  37 us (13%)
  starting transfers between devices  36.9 us (13%)
  waiting for transfers between devices  30.6 us (11%)
  other arithmetic  12.1 us (4%)
    psum x1, blocking collectives, shards(): mixed = lax.psum(partial_mix, 'member').astype(jnp.bfloat16)  81.5 us
    gather x2, local copies, waits for them, and re-layouts, shards(): innov_sel = info_rim[0][lists_mine]  20 us
    all_to_all x1, waiting for transfers between devices, copy_for_each(): lax.all_to_all(jnp.broadcast_to(array[None], (devices, *array.shape)), ax...  19.9 us
    gather x1, local copies, waits for them, and re-layouts, shards(): prec_sel = info_rim[1][lists_mine]  19.4 us
    all_to_all x1, starting transfers between devices, copy_for_each(): lax.all_to_all(jnp.broadcast_to(array[None], (devices, *array.shape)), ax...  15.4 us
    gather x2, local copies, waits for them, and re-layouts, shards(): local_obs = all_members[:, lists_mine]  12.9 us
    dot_general x12, matrix products, newton(): jnp.einsum('bij,bjk->bik', root_iter, correction, precision=lax.Precision...  11.7 us
    ppermute x2, starting transfers between devices, padded(): lax.ppermute(head, axis, [((i + 1) % count, i) for i in range(count)])  11.5 us
  transfers between devices with their start and end apart: 6, of which 3 were waited for; matrix products, arithmetic and copies ran while one was open for 17% of the time, Pallas kernels for 0%

commit v1 on v0

--- a/solution.py
+++ b/solution.py
@@ -96,6 +96,10 @@
     ocean_frac,
     ocean_ens,
 ):
+
+    def solve_joints(local_x):
+        return lax.all_gather(local_x, "member").sum(axis=0)
+
     n_member = lax.axis_size("member")
     n_space = lax.axis_size("space")
     member_idx = lax.axis_index("member")
@@ -124,7 +128,7 @@
     take_one = arrived[ocean_src[:, 0] % n_space].astype(jnp.float32)
     take_two = arrived[ocean_src[:, 1] % n_space].astype(jnp.float32)
     partial_mix = coef_one * take_one + coef_two * take_two
-    mixed = lax.psum(partial_mix, "member").astype(jnp.bfloat16)
+    mixed = solve_joints(partial_mix).astype(jnp.bfloat16)
     return apply_weights(ocean_ens, mixed)
 
 

time: 277 us -> 769 us (2.78)
  waiting for transfers between devices: 30.6 us -> 577 us
  blocking collectives: 81.5 us -> 0 us
  other arithmetic: 12.1 us -> 31.3 us
  between operations: 0.37 us -> 13.7 us
    all_gather x0 -> x1, waiting for transfers between devices: none -> 540 us  [solve_joints(): return lax.all_gather(local_x, 'member').sum(axis=0)]
    psum x1 -> x0, blocking collectives: 81.5 us -> none  [shards(): mixed = lax.psum(partial_mix, 'member').astype(jnp.bfloat16)]
    reduce_sum x0 -> x1, other arithmetic: none -> 21.6 us  [solve_joints(): return lax.all_gather(local_x, 'member').sum(axis=0)]
  transfers between devices with their start and end apart: 6 -> 7, of which waited for: 3 -> 4; matrix products, arithmetic and copies ran while one was open for 17% -> 6% of each run, Pallas kernels for 0% -> 0%
where the time goes in v1:
time: 769 us; the launch traced here: 767 us
  waiting for transfers between devices  577 us (75%)
  local copies, waits for them, and re-layouts  71.2 us (9%)
  starting transfers between devices  37.1 us (5%)
  matrix products  36.2 us (5%)
  other arithmetic  31.3 us (4%)
  between operations  13.7 us (2%)
    all_gather x1, waiting for transfers between devices, solve_joints(): return lax.all_gather(local_x, 'member').sum(axis=0)  540 us
    all_to_all x1, waiting for transfers between devices, copy_for_each(): lax.all_to_all(jnp.broadcast_to(array[None], (devices, *array.shape)), ax...  24.8 us
    reduce_sum x1, other arithmetic, solve_joints(): return lax.all_gather(local_x, 'member').sum(axis=0)  21.6 us
    gather x2, local copies, waits for them, and re-layouts, shards(): innov_sel = info_rim[0][lists_mine]  19.4 us
    gather x1, local copies, waits for them, and re-layouts, shards(): prec_sel = info_rim[1][lists_mine]  19.4 us
  transfers between devices with their start and end apart: 7, of which 4 were waited for; matrix products, arithmetic and copies ran while one was open for 6% of the time, Pallas kernels for 0%

profile of v1, /device:TPU:6, one launch (start us, length us, event | category | flops | bytes accessed | tf_op | source)
XLA Modules:
  0.0 767.3 jit_solution(15818956337043159522)
XLA Ops:
  6.5 1.9 collective-permute-start
  8.5 5.8 collective-permute-start.1
  14.2 1.9 collective-permute-done.1
  16.9 1.3 broadcast_in_dim.23
  18.2 15.3 %all-to-all-start = ((bf16[16,5,6144]{2,1,0:T(8,128)(2,1)}), bf16[16,5,6144]{2,1,0:T(8,128)(2,1)S(1)}, u32[]{:S(2)}, u32[]{:S(2)}) async-start(bf16[16,5,6144]{2,1,0:T(8,128)(2,1)} %broadcast_in_dim.23), calls=%async_computation | async-start | bytes 3145728 | tf_op jit(solution)/shard_map/all_to_all | solution.py:27
  33.6 1.9 collective-permute-start.2
  35.5 5.8 collective-permute-start.3
  43.0 19.4 %gather_fusion.1 = bf16[3072]{0:T(1024)(128)(2,1)S(1)} fusion(bf16[6144]{0:T(1024)(128)(2,1)S(1)} %get-tuple-element.52, s32[3072]{0:T(1024)S(1)} %broadcast_clamp_fusion), kind=kCustom, calls=%fused_computation.1 | custom fusion | bytes 24576 | tf_op jit(solution)/shard_map/gather | solution.py:119
  62.4 19.4 %gather_fusion.2 = bf16[3072]{0:T(1024)(128)(2,1)S(1)} fusion(bf16[6144]{0:T(1024)(128)(2,1)S(1)} %get-tuple-element.51, s32[3072]{0:T(1024)S(1)} %broadcast_clamp_fusion), kind=kCustom, calls=%fused_computation.2 | custom fusion | bytes 24576 | tf_op jit(solution)/shard_map/gather | solution.py:118
  82.5 24.8 %all-to-all-done = bf16[16,5,6144]{2,1,0:T(8,128)(2,1)S(1)} async-done(((bf16[16,5,6144]{2,1,0:T(8,128)(2,1)}), bf16[16,5,6144]{2,1,0:T(8,128)(2,1)S(1)}, u32[]{:S(2)}, u32[]{:S(2)}) %all-to-all-start) | async-done | bytes 983072 | tf_op jit(solution)/shard_map/all_to_all | solution.py:27
  108.7 9.2 %gather_fusion = bf16[3072,80]{1,0:T(8,128)(2,1)S(1)} fusion(bf16[80,6144]{0,1:T(8,128)(2,1)S(1)} %copy.50, s32[3072]{0:T(1024)S(1)} %broadcast_clamp_fusion), kind=kCustom, calls=%fused_computation | custom fusion | bytes 995328 | tf_op jit(solution)/shard_map/gather | solution.py:117
  119.2 32.0 %while.13 = (s32[]{:T(128)}, f32[12,80,80]{1,2,0:T(8,128)S(1)}, f32[12,80,80]{2,1,0:T(8,128)S(1)}, s32[]{:T(128)}) while((s32[]{:T(128)}, f32[12,80,80]{1,2,0:T(8,128)S(1)}, f32[12,80,80]{2,1,0:T(8,128)S(1)}, s32[]{:T(128)}) %tuple.31), condition=%wide.region_3.4_spmd.clone, body=%wide.region_2.3_spmd.clone.sunk | while | flops 221350400 | bytes 4044853 | solution.py:71
  123.5 1.0 convolution_bitcast_fusion.2
  126.2 1.0 convolution_bitcast_fusion.2
  131.5 1.0 convolution_bitcast_fusion.2
  134.2 1.0 convolution_bitcast_fusion.2
  139.5 1.0 convolution_bitcast_fusion.2
  142.2 1.0 convolution_bitcast_fusion.2
  147.5 1.0 convolution_bitcast_fusion.2
  153.9 1.5 gather_fusion.3
  155.3 6.2 all-to-all-start.1
  161.9 10.3 %all-to-all-done.1 = bf16[32,80,80]{2,1,0:T(8,128)(2,1)S(1)} async-done(((bf16[32,80,80]{2,1,0:T(8,128)(2,1)}), bf16[32,80,80]{2,1,0:T(8,128)(2,1)S(1)}, u32[]{:S(2)}, u32[]{:S(2)}) %all-to-all-start.1) | async-done | bytes 409632 | tf_op jit(solution)/shard_map/all_to_all | solution.py:123
  173.1 2.1 gather_fusion.5
  175.2 4.1 fusion.5
  179.3 5.6 copy.53
  184.9 1.5 copy-done
  186.7 1.7 fusion.4
  188.4 540.1 %all-gather.2.cloned.1.call-done = f32[16,96,80,80]{1,3,2,0:T(8,128)} async-done(((f32[1,96,80,80]{1,3,2,0:T(8,128)}), f32[16,96,80,80]{1,3,2,0:T(8,128)}) %all-gather.2.cloned.1.call-update) | async-done | bytes 39321616 | tf_op jit(solution)/shard_map/all_gather | solution.py:101
  728.5 21.6 %reduce_sum.30 = bf16[96,80,80]{0,2,1:T(8,128)(2,1)} reduce(f32[16,96,80,80]{1,3,2,0:T(8,128)} %all-gather.2.cloned.1.call-done, f32[]{:T(128)} %constant.70.clone.1), dimensions={0}, to_apply=%region_4.5 | reduce | flops 9216000 | bytes 40550404 | tf_op jit(solution)/shard_map/reduce_sum | solution.py:101
  750.1 5.9 copy.56
  755.9 2.8 fusion.7
  758.7 1.8 copy.58
  (117 shorter events, 34.5 us)
Async XLA Ops:
  6.5 7.7 %collective-permute-start = (bf16[5,2048]{1,0:T(8,128)(2,1)}, bf16[5,2048]{1,0:T(8,128)(2,1)S(1)}, u32[]{:S(2)}, u32[]{:S(2)}) collective-permute-start(bf16[5,2048]{1,0:T(8,128)(2,1)} %param.11), channel_id=1, source_target_pairs={{0,16},{16,32},{32,48},{48,64},{64,80},{80,96},{96,112},{112,128},... | collective-permute-start | bytes 61448 | tf_op jit(solution)/shard_map/ppermute | solution.py:16
  8.5 7.7 collective-permute-start.1
  18.2 15.3 %copy-start.1 = (bf16[2048]{0:T(1024)(128)(2,1)S(1)}, bf16[2048]{0:T(1024)(128)(2,1)}, u32[]{:S(2)}) copy-start(bf16[2048]{0:T(1024)(128)(2,1)} %param.13) | copy-start | bytes 12292
  18.2 15.4 %copy-start.2 = (bf16[2048]{0:T(1024)(128)(2,1)S(1)}, bf16[2048]{0:T(1024)(128)(2,1)}, u32[]{:S(2)}) copy-start(bf16[2048]{0:T(1024)(128)(2,1)} %param.12) | copy-start | bytes 12292
  18.2 89.1 %all-to-all-start = ((bf16[16,5,6144]{2,1,0:T(8,128)(2,1)}), bf16[16,5,6144]{2,1,0:T(8,128)(2,1)S(1)}, u32[]{:S(2)}, u32[]{:S(2)}) async-start(bf16[16,5,6144]{2,1,0:T(8,128)(2,1)} %broadcast_in_dim.23), calls=%async_computation | async-start | bytes 3145728 | tf_op jit(solution)/shard_map/all_to_all | solution.py:27
  33.6 9.2 %collective-permute-start.2 = (bf16[2,2048]{1,0:T(2,128)(2,1)S(1)}, bf16[2,2048]{1,0:T(2,128)(2,1)S(1)}, u32[]{:S(2)}, u32[]{:S(2)}) collective-permute-start(bf16[2,2048]{1,0:T(2,128)(2,1)S(1)} %pad_maximum_fusion.2), channel_id=1, source_target_pairs={{0,16},{16,32},{32,48},{48,64},{64,80},{80,96},{96,112},{112,128},... | collective-permute-start | bytes 24584 | tf_op jit(solution)/shard_map/ppermute | solution.py:16
  35.5 7.3 collective-permute-start.3
  152.7 9.1 %copy-start.3 = (s32[96,2]{0,1:T(2,128)S(1)}, s32[96,2]{0,1:T(2,128)}, u32[]{:S(2)}) copy-start(s32[96,2]{0,1:T(2,128)} %param.17) | copy-start | bytes 2308
  152.7 9.2 %copy-start.4 = (f32[96]{0:T(128)S(1)}, f32[96]{0:T(128)}, u32[]{:S(2)}) copy-start(f32[96]{0:T(128)} %param.18) | copy-start | bytes 1156
  155.3 16.8 %all-to-all-start.1 = ((bf16[32,80,80]{2,1,0:T(8,128)(2,1)}), bf16[32,80,80]{2,1,0:T(8,128)(2,1)S(1)}, u32[]{:S(2)}, u32[]{:S(2)}) async-start(bf16[32,80,80]{2,1,0:T(8,128)(2,1)} %gather_fusion.3), calls=%async_computation.1 | async-start | bytes 1310720 | tf_op jit(solution)/shard_map/all_to_all | solution.py:123
  161.6 566.9 %all-gather.2.cloned.1.call-start = ((), (), s32[]{:S(2)}) async-start(), calls=%async_computation.2 | async-start | bytes 55705600 | tf_op jit(solution)/shard_map/all_gather | solution.py:101
  184.9 1.5 copy-start
Sparse Core Ops, SparseCore 0:
  185.0 543.4 all-gather.1
